TPU v7x, 32 devices: a whole 2x2x4 slice. The times are simulated.
32 devices in a mesh: node: 4 (over y, core), rep: 8 (over z, x).
Axes of the slice: x: 2, y: 2, z: 4, core: 2. Of those that a mesh axis runs over, the one named last changes fastest.
Arguments:
- tokens: bfloat16 [8192, 2048], P(('node', 'rep')), may hold values from -60 to 60
- cotangent: bfloat16 [8192, 512], P(('node', 'rep')), may hold values from -6 to 6
- value_weight: bfloat16 [2048, 512], P('node'), may hold values from -0.25 to 0.25
Outputs:
- input_grad: bfloat16 [8192, 2048], P(('node', 'rep'))
- update: float32 [2048, 512], P('node')
All inputs are finite; a program needn't handle non-finite values.
Results may differ from a plain program's by a relative error of at most 0.025.
Values may be sent and summed in bfloat16 or wider, within the bound.
A program may use at most 64 MiB of HBM per device.

v0:
```python
import functools
import math

import jax
import jax.numpy as jnp
from jax import lax
from jax.experimental import pallas as pl
from jax.experimental.pallas import tpu as pltpu
from jax.sharding import PartitionSpec as P

HD = 128
NS_ITERS = 5
NSUB = 2
TILE_ROWS = 16

coef_a = 3.4445
coef_b = -4.775
coef_c = 2.0315
epsilon = 1e-07

MESH = pl.DeviceIdType.MESH
F32, BF16 = jnp.float32, jnp.bfloat16


def mm_t(a, b):
    return lax.dot_general(a, b, (((0,), (0,)), ((), ())), preferred_element_type=F32)


def parts_of(a):
    hi = a.astype(BF16)
    lo = (a - hi.astype(F32)).astype(BF16)
    return hi, lo


def left_form(a):
    return jnp.concatenate(parts_of(a), axis=1)


def right_form(b):
    row = jnp.concatenate(parts_of(b), axis=1)
    return jnp.concatenate([row, row], axis=0)


def product(left, right):
    n = right.shape[1] // 2
    wide = jnp.dot(left, right, preferred_element_type=F32)
    return wide[:, :n] + wide[:, n:]


def kernel(cfg, tok_hbm, cot_hbm, w_hbm, igbuf, rows_ref, form_ref, tok_ref, cot_ref, w_ref, tokx, cotx, wall, acc1, away1, send1, recv1, send2,
           recv2, zsend, zrecv, grad, early, gram_own, gram_in, lsem, ssem, rsem):
    depth, width, heads, zs = cfg
    din = tok_ref.shape[1]
    tokens = tok_ref.shape[0]
    block = din // 4
    half, quarter = block // 2, block // 4
    piece = quarter // zs
    cw = width // NSUB

    node, rep = lax.axis_index("node"), lax.axis_index("rep")
    y, c = node // 2, node % 2
    z, x = rep // 2, rep % 2
    partner = (y * 2 + 1 - c, rep)
    y_peer = ((1 - y) * 2 + c, rep)
    x_peer = (node, z * 2 + 1 - x)
    z_of = [(z + d) % zs for d in range(zs)]
    z_peer = [(node, z_of[d] * 2 + x) for d in range(zs)]

    counts = [0]
    sends = []

    def remote(src, dst, peer):
        k = counts[0]
        counts[0] += 1
        cp = pltpu.make_async_remote_copy(src_ref=src, dst_ref=dst, send_sem=ssem.at[k], recv_sem=rsem.at[k],
                                          device_id=peer, device_id_type=MESH)
        cp.start()
        sends.append(cp)
        return cp

    def col(p, core, start=0, size=block):
        return pl.ds(pl.multiple_of((2 * p + core) * block + start, size), size)

    own_w = pl.ds(pl.multiple_of(node * block, block), block)

    pairs = ((cot_hbm, cot_ref), (tok_hbm, tok_ref), (w_hbm, w_ref))
    loads = [pltpu.make_async_copy(src, dst, lsem.at[i]) for i, (src, dst) in enumerate(pairs)]
    for cp in loads:
        cp.start()

    barrier = pltpu.get_barrier_semaphore()
    peers = [partner, y_peer, x_peer] + z_peer[1:]
    for peer in peers:
        pl.semaphore_signal(barrier, inc=1, device_id=peer, device_id_type=MESH)
    pl.semaphore_wait(barrier, len(peers))

    for cp in loads[:2]:
        cp.wait()
    first = [remote(cot_ref, cotx, partner)]
    first += [remote(tok_ref.at[:, col(p, 1 - c)], tokx.at[p], partner) for p in range(2)]

    def w_part(n, side, i):
        return pl.ds(pl.multiple_of(n * block + side * half + i * quarter, quarter), quarter)

    def send_w(i):
        rows = pl.ds(pl.multiple_of(x * half + i * quarter, quarter), quarter)
        return remote(w_ref.at[rows], wall.at[w_part(node, x, i)], y_peer)

    def relay_w(i):
        rows = w_part((1 - y) * 2 + c, x, i)
        return remote(wall.at[rows], wall.at[rows], x_peer)

    loads[2].wait()
    w_y = [send_w(0)]

    def dim(p, level):
        return (y, y_peer) if (p + level) % 2 == 0 else (x, x_peer)

    chunks = [(p, s) for s in range(NSUB) for p in range(2)]

    def cs(s):
        return pl.ds(s * cw, cw)

    def chip_sum(p, start):
        mine = mm_t(tok_ref[:, col(p, c, start, half)], cot_ref[...])
        return mine, pl.ds(pl.multiple_of(start, half), half)

    mine = {}
    for p in range(2):
        start = (1 - dim(p, 0)[0]) * half
        away1[p], mine[p] = chip_sum(p, start)
    st1, st2, stz, sg, sg2, sg1 = {}, {}, {}, {}, {}, {}
    first[0].wait_recv()
    for p in range(2):
        first[1 + p].wait_recv()
        send1[p] = (away1[p] + mm_t(tokx[p, :, mine[p]], cotx[...])).astype(BF16)
        for s in range(NSUB):
            st1[p, s] = remote(send1.at[p, :, cs(s)], recv1.at[p, :, cs(s)], dim(p, 0)[1])
    w_partner = remote(w_ref, wall.at[own_w], partner)
    for p in range(2):
        value, here = chip_sum(p, dim(p, 0)[0] * half)
        acc1[p] = value + mm_t(tokx[p, :, here], cotx[...])

    def input_rows(n, rows_of_w):
        rows = pl.ds(pl.multiple_of(n * block, block), block)
        out = lax.dot_general(cot_ref[...], rows_of_w, (((1,), (1,)), ((), ())), preferred_element_type=F32)
        igbuf[:, rows] = out.astype(BF16)

    def gathered(n):
        return wall[pl.ds(pl.multiple_of(n * block, block), block), :]

    input_rows(node, w_ref[...])
    w_partner.wait_recv()
    input_rows(y * 2 + 1 - c, gathered(y * 2 + 1 - c))

    for p, s in chunks:
        st1[p, s].wait_recv()
        bit, peer = dim(p, 1)
        away = pl.ds(pl.multiple_of((1 - bit) * quarter, quarter), quarter)
        keep = pl.ds(pl.multiple_of(bit * quarter, quarter), quarter)
        send2[p, :, cs(s)] = (acc1[p, away, cs(s)] + recv1[p, away, cs(s)].astype(F32)).astype(BF16)
        st2[p, s] = remote(send2.at[p, :, cs(s)], recv2.at[p, :, cs(s)], peer)
        acc1[p, keep, cs(s)] = acc1[p, keep, cs(s)] + recv1[p, keep, cs(s)].astype(F32)
    w_y.append(send_w(1))
    w_y[0].wait_recv()
    w_x = [relay_w(0)]

    for p, s in chunks:
        st2[p, s].wait_recv()
        bit, peer = dim(p, 1)
        keep = pl.ds(pl.multiple_of(bit * quarter, quarter), quarter)
        total = acc1[p, keep, cs(s)] + recv2[p, :, cs(s)].astype(F32)
        acc1[p, keep, cs(s)] = total
        zsend[p, :, cs(s)] = total.astype(BF16)
        cps = []
        for d in range(1, zs):
            rows = pl.ds(pl.multiple_of(z_of[d] * piece, piece), piece)
            cps.append(remote(zsend.at[p, rows, cs(s)], zrecv.at[p, d - 1, :, cs(s)], z_peer[d]))
        stz[p, s] = cps

    for p, s in chunks:
        b0, _ = dim(p, 0)
        b1, _ = dim(p, 1)
        mine = pl.ds(pl.multiple_of(b1 * quarter + z * piece, piece), piece)
        total = acc1[p, mine, cs(s)]
        for d in range(1, zs):
            stz[p, s][d - 1].wait_recv()
            total = total + zrecv[p, d - 1, :, cs(s)].astype(F32)
        rows = pl.ds(pl.multiple_of(b0 * half + b1 * quarter + z * piece, piece), piece)
        grad[p, rows, cs(s)] = total.astype(BF16)
        sg[p, s] = [remote(grad.at[p, rows, cs(s)], grad.at[p, rows, cs(s)], z_peer[d]) for d in range(1, zs)]

    w_y[1].wait_recv()
    w_x.append(relay_w(1))
    for p, s in chunks:
        for cp in sg[p, s]:
            cp.wait_recv()
        b0, _ = dim(p, 0)
        b1, peer = dim(p, 1)
        rows = pl.ds(pl.multiple_of(b0 * half + b1 * quarter, quarter), quarter)
        sg2[p, s] = remote(grad.at[p, rows, cs(s)], grad.at[p, rows, cs(s)], peer)
    for cp in w_x:
        cp.wait_recv()
    y_w = pl.ds(pl.multiple_of(((1 - y) * 2 + c) * block, block), block)
    w_fwd = remote(wall.at[y_w], wall.at[y_w], partner)
    for p, s in chunks:
        sg2[p, s].wait_recv()
        b0, peer = dim(p, 0)
        rows = pl.ds(pl.multiple_of(b0 * half, half), half)
        sg1[p, s] = remote(grad.at[p, rows, cs(s)], grad.at[p, rows, cs(s)], peer)

    input_rows((1 - y) * 2 + c, gathered((1 - y) * 2 + c))
    w_fwd.wait_recv()
    input_rows((1 - y) * 2 + 1 - c, gathered((1 - y) * 2 + 1 - c))

    def gram_of(h, p, bit):
        rows = pl.ds(pl.multiple_of(bit * half, half), half)
        g = grad[p, rows, h * HD:(h + 1) * HD]
        return mm_t(g, g)

    for h in range(heads):
        early[0, h] = gram_of(h, 0, y)
        early[1, h] = gram_of(h, 1, x)
    per_sub = heads // NSUB
    cp_gram = []
    for s in range(NSUB):
        for p in range(2):
            sg1[p, s].wait_recv()
        for h in range(s * per_sub, (s + 1) * per_sub):
            gram_own[h] = (early[0, h] + gram_of(h, 0, 1 - y)) + (early[1, h] + gram_of(h, 1, 1 - x))
        these = pl.ds(s * per_sub, per_sub)
        cp_gram.append(remote(gram_own.at[these], gram_in.at[these], partner))
    rows_ref[...] = grad[y]
    for cp in cp_gram:
        cp.wait_recv()

    ii = lax.broadcasted_iota(jnp.int32, (HD, HD), 0)
    jj = lax.broadcasted_iota(jnp.int32, (HD, HD), 1)
    eye = (ii == jj).astype(F32)
    grams, totals, scales = [], [None] * heads, []
    for h in range(heads):
        raw = gram_own[h] + gram_in[h]
        squares = jnp.sum(jnp.sum(raw * eye, axis=1, keepdims=True), axis=0, keepdims=True)
        inverse = 1.0 / (jnp.sqrt(squares) + epsilon)
        scales.append(inverse)
        grams.append(raw * inverse * inverse)
    for step in range(NS_ITERS):
        rights = [right_form(g) for g in grams]
        squared = [product(left_form(g), r) for g, r in zip(grams, rights)]
        factors = [coef_a * eye + coef_b * g + coef_c * q for g, q in zip(grams, squared)]
        forms = [right_form(f) for f in factors]
        if step + 1 < NS_ITERS:
            halfway = [product(left_form(g), f) for g, f in zip(grams, forms)]
        if step == 0:
            totals = factors
        else:
            totals = [product(left_form(t), f) for t, f in zip(totals, forms)]
        if step + 1 < NS_ITERS:
            grams = [product(left_form(g), f) for g, f in zip(halfway, forms)]

    for h in range(heads):
        scaled = totals[h] * (scales[h] * (0.2 * math.sqrt(din)))
        form_ref[h] = jnp.concatenate(parts_of(scaled), axis=1)
    for cp in sends:
        cp.wait_send()


def finish(ig_ref, rows_ref, form_ref, ig_out, up_out, upbuf, sems):
    heads = form_ref.shape[0]
    step = upbuf.shape[0] // 4
    copies = [pltpu.make_async_copy(ig_ref, ig_out, sems.at[0])]
    copies[0].start()
    for i in range(4):
        part = pl.ds(i * step, step)
        for h in range(heads):
            cols = pl.ds(h * HD, HD)
            upbuf[part, cols] = product(rows_ref[part, cols], form_ref[h])
        copies.append(pltpu.make_async_copy(upbuf.at[part], up_out.at[part], sems.at[i + 1]))
        copies[-1].start()
    for cp in copies:
        cp.wait()


def fused(tokens, cotangent, value_weight, zs):
    tok, din = tokens.shape
    width = cotangent.shape[1]
    heads = width // HD
    block = din // 4
    half, quarter = block // 2, block // 4
    piece = quarter // zs
    nrem = 4 + 2 * NSUB * (1 + 1 + 2 * (zs - 1) + 1 + 1) + 6 + NSUB
    vm = pltpu.VMEM
    held = pl.pallas_call(
        functools.partial(kernel, (tok, width, heads, zs)),
        out_shape=(
            jax.ShapeDtypeStruct((tok, din), BF16),
            jax.ShapeDtypeStruct((block, width), BF16),
            jax.ShapeDtypeStruct((heads, HD, 2 * HD), BF16),
        ),
        in_specs=[pl.BlockSpec(memory_space=pl.ANY)] * 3,
        out_specs=(pl.BlockSpec(memory_space=pltpu.VMEM),) * 3,
        scratch_shapes=[
            vm((tok, din), BF16),
            vm((tok, width), BF16),
            vm((block, width), BF16),
            vm((2, tok, block), BF16),
            vm((tok, width), BF16),
            vm((din, width), BF16),
            vm((2, half, width), F32),
            vm((2, half, width), F32),
            vm((2, half, width), BF16),
            vm((2, half, width), BF16),
            vm((2, quarter, width), BF16),
            vm((2, quarter, width), BF16),
            vm((2, quarter, width), BF16),
            vm((2, zs - 1, piece, width), BF16),
            vm((2, block, width), BF16),
            vm((2, heads, HD, HD), F32),
            vm((heads, HD, HD), F32),
            vm((heads, HD, HD), F32),
            pltpu.SemaphoreType.DMA((3,)),
            pltpu.SemaphoreType.DMA((nrem,)),
            pltpu.SemaphoreType.DMA((nrem,)),
        ],
        compiler_params=pltpu.CompilerParams(collective_id=0, has_side_effects=True, vmem_limit_bytes=24 * 1024 * 1024),
    )(*(pltpu.with_memory_space_constraint(a, pltpu.HBM) for a in (tokens, cotangent, value_weight)))
    return pl.pallas_call(
        finish,
        out_shape=(jax.ShapeDtypeStruct((tok, din), BF16), jax.ShapeDtypeStruct((block, width), F32)),
        in_specs=[pl.BlockSpec(memory_space=pltpu.VMEM)] * 3,
        out_specs=(pl.BlockSpec(memory_space=pltpu.HBM),) * 2,
        scratch_shapes=[vm((block, width), F32), pltpu.SemaphoreType.DMA((5,))],
        compiler_params=pltpu.CompilerParams(vmem_limit_bytes=8 * 1024 * 1024),
    )(*held)


def general(tokens, cotangent, value_weight):
    width = value_weight.shape[1]
    din = tokens.shape[1]
    local_rows = value_weight.shape[0]
    heads = width // HD
    input_grad = lax.dot_general(
        cotangent,
        lax.all_gather(value_weight, "node", axis=0, tiled=True),
        (((1,), (1,)), ((), ())),
        preferred_element_type=F32,
    ).astype(BF16)
    partial_rows = lax.psum_scatter(
        lax.dot_general(tokens, cotangent, (((0,), (0,)), ((), ())), preferred_element_type=F32).astype(BF16),
        "node",
        scatter_dimension=0,
        tiled=True,
    ).astype(F32)
    gradient = lax.psum(partial_rows, "rep")
    blocks = gradient.reshape(local_rows, heads, HD)
    exact = functools.partial(jnp.einsum, precision=lax.Precision.HIGHEST)
    gram_raw = lax.psum(exact("rhi,rhj->hij", blocks, blocks), "node")
    divisor = jnp.sqrt(jnp.einsum("hii->h", gram_raw)) + epsilon
    gram = gram_raw / (divisor * divisor)[:, None, None]
    identity = jnp.broadcast_to(jnp.eye(HD, dtype=F32), (heads, HD, HD))
    total = identity
    for step in range(NS_ITERS):
        factor = coef_a * identity + coef_b * gram + coef_c * exact("hij,hjk->hik", gram, gram)
        total = exact("hij,hjk->hik", total, factor)
        if step + 1 < NS_ITERS:
            gram = exact("hji,hjk->hik", factor, exact("hij,hjk->hik", gram, factor))
    iterate = exact("rhi,hij->rhj", blocks / divisor[None, :, None], total)
    return input_grad, 0.2 * math.sqrt(din) * iterate.reshape(local_rows, width)


def solution(mesh):
    nodes, reps = mesh.shape["node"], mesh.shape["rep"]

    def per_device(tokens, cotangent, value_weight):
        zs = reps // 2
        pieces = nodes * 4 * zs
        fits = nodes == 4 and reps % 2 == 0 and zs > 1 and tokens.shape[1] % (pieces * TILE_ROWS) == 0
        if fits:
            return fused(tokens, cotangent, value_weight, zs)
        return general(tokens, cotangent, value_weight)

    return jax.shard_map(
        per_device,
        mesh=mesh,
        in_specs=(P(("node", "rep"), None), P(("node", "rep"), None), P("node", None)),
        out_specs=(P(("node", "rep"), None), P("node", None)),
        check_vma=False,
    )
```

profile of v0, /device:TPU:1, one launch (start us, length us, event | category | flops | bytes accessed | tf_op | source)
XLA Modules:
  0.0 44.5 jit_solution(10596087759508469810)
XLA Ops:
  0.6 42.5 %shard_map.50 = (bf16[256,2048]{1,0:T(8,128)(2,1)S(1)}, bf16[512,512]{1,0:T(8,128)(2,1)S(1)}, bf16[4,128,256]{2,1,0:T(8,128)(2,1)S(1)}) custom-call(bf16[256,2048]{1,0:T(8,128)(2,1)} %tok_hbm.1, bf16[256,512]{1,0:T(8,128)(2,1)} %cot_hbm.1, bf16[512,512]{1,0:T(8,128)(2,1)} %w_hbm.1), custom_call_target="tpu_custom_call" | custom-call | tf_op jit(solution)/shard_map/pallas_call | solution.py:293
  43.2 1.4 %shard_map.51 = (bf16[256,2048]{1,0:T(8,128)(2,1)}, f32[512,512]{1,0:T(8,128)}) custom-call(bf16[256,2048]{1,0:T(8,128)(2,1)S(1)} %get-tuple-element.5.ig_ref, bf16[512,512]{1,0:T(8,128)(2,1)S(1)} %get-tuple-element.6.rows_ref, bf16[4,128,256]{2,1,0:T(8,128)(2,1)S(1)} %get-tuple-element.7.form_ref), custom_call_target="tpu_custom_call" | custom-call | tf_op jit(solution)/shard_map/pallas_call | solution.py:327
where the time goes:
time: 44.7 us; the launch traced here: 44.5 us
  Pallas kernels  43.9 us (98%)
  between operations  0.64 us (1%)
    pallas_call x1, Pallas kernels, fused(): pl.pallas_call(functools.partial(kernel, (tok, width, heads, zs)), out_sh...  42.5 us
    pallas_call x1, Pallas kernels, fused(): pl.pallas_call(finish, out_shape=(jax.ShapeDtypeStruct((tok, din), BF16),...  1.36 us

commit v1 on v0

v1 whole, which is shorter than its diff:
```python
import functools
import math

import jax
import jax.numpy as jnp
from jax import lax
from jax.experimental import pallas as pl
from jax.experimental.pallas import tpu as pltpu
from jax.sharding import PartitionSpec as P

HD = 128
NS_ITERS = 5
WPARTS = 8
W_EARLY = 1
ORDER = ("z0", "z1", "z2", "r0", "z3", "f1", "r1", "f2", "r2", "f3", "l0", "r3", "l1", "g0", "l2", "g1", "e0", "l3", "g2", "e1", "g3", "w", "e2", "e3", "i", "o0", "o1", "o2", "o3")

coef_a = 3.4445
coef_b = -4.775
coef_c = 2.0315
epsilon = 1e-07

MESH = pl.DeviceIdType.MESH
F32, BF16 = jnp.float32, jnp.bfloat16


def mm_t(a, b):
    return lax.dot_general(a, b, (((0,), (0,)), ((), ())), preferred_element_type=F32)


def parts_of(a):
    hi = a.astype(BF16)
    lo = (a - hi.astype(F32)).astype(BF16)
    return hi, lo


def left_form(a):
    return jnp.concatenate(parts_of(a), axis=1)


def right_form(b):
    row = jnp.concatenate(parts_of(b), axis=1)
    return jnp.concatenate([row, row], axis=0)


def product(left, right):
    n = right.shape[1] // 2
    wide = jnp.dot(left, right, preferred_element_type=F32)
    return wide[:, :n] + wide[:, n:]


def kernel(cfg, tok_hbm, cot_hbm, w_hbm, igbuf, rows_ref, form_ref, tok_ref, cot_ref, w_ref, tokx, cotx, wall, acc, send1, recv1, send2,
           recv2, zsend, zrecv, grad, early, gram_own, gram_in, lsem, ssem, rsem):
    width, heads, zs = cfg
    din = tok_ref.shape[1]
    block = din // 4
    half, quarter = block // 2, block // 4
    wpart = block // WPARTS

    node, rep = lax.axis_index("node"), lax.axis_index("rep")
    y, c = node // 2, node % 2
    z, x = rep // 2, rep % 2
    partner = (y * 2 + 1 - c, rep)
    y_peer = ((1 - y) * 2 + c, rep)
    x_peer = (node, z * 2 + 1 - x)
    z_others = [(node, lax.rem(z + d, zs) * 2 + x) for d in range(1, zs)]
    bits = [(y, x), (x, y)]
    towards = [(y_peer, x_peer), (x_peer, y_peer)]
    roots = [zs // 2 - 1 + p for p in range(2)]

    names = {}

    def sem(of, name):
        return of.at[names.setdefault((id(of), name), sum(1 for key in names if key[0] == id(of)))]

    def copy_to(src, dst, peer, out, into):
        return pltpu.make_async_remote_copy(src_ref=src, dst_ref=dst, send_sem=sem(ssem, out), recv_sem=sem(rsem, into),
                                            device_id=peer, device_id_type=MESH)

    def remote(src, dst, peer, out, into):
        cp = copy_to(src, dst, peer, out, into)
        cp.start()
        return cp

    def received(ref, into):
        pltpu.make_async_remote_copy(src_ref=ref, dst_ref=ref, send_sem=ssem.at[0], recv_sem=sem(rsem, into),
                                     device_id=partner, device_id_type=MESH).wait_recv()

    def sent(ref, out):
        pltpu.make_async_remote_copy(src_ref=ref, dst_ref=ref, send_sem=sem(ssem, out), recv_sem=rsem.at[0],
                                     device_id=partner, device_id_type=MESH).wait_send()

    def start_of(p, i):
        b0, b1 = bits[p]
        h = 1 - b0 if i < 2 else b0
        q = 1 - b1 if i % 2 == 0 else b1
        return h * half + q * quarter

    def quarter_rows(p, i):
        return pl.ds(pl.multiple_of(start_of(p, i), quarter), quarter)

    def col(p, core, i):
        return pl.ds(pl.multiple_of((2 * p + core) * block + start_of(p, i), quarter), quarter)

    own_w = pl.ds(pl.multiple_of(node * block, block), block)

    pairs = ((cot_hbm, cot_ref), (tok_hbm, tok_ref), (w_hbm, w_ref))
    loads = [pltpu.make_async_copy(src, dst, lsem.at[i]) for i, (src, dst) in enumerate(pairs)]
    for cp in loads:
        cp.start()

    barrier = pltpu.get_barrier_semaphore()
    peers = [partner, y_peer, x_peer] + z_others
    for peer in peers:
        pl.semaphore_signal(barrier, inc=1, device_id=peer, device_id_type=MESH)
    pl.semaphore_wait(barrier, len(peers))

    for cp in loads[:2]:
        cp.wait()
    remote(cot_ref, cotx, partner, "cot", "cot")
    for i in range(4):
        for p in range(2):
            remote(tok_ref.at[:, col(p, 1 - c, i)], tokx.at[p, :, quarter_rows(p, i)], partner, "tok", f"tok{i}")
    loads[2].wait()

    def w_part(n, side, i):
        return pl.ds(pl.multiple_of(n * block + side * half + i * wpart, wpart), wpart)

    def send_w(i):
        rows = pl.ds(pl.multiple_of(x * half + i * wpart, wpart), wpart)
        remote(w_ref.at[rows], wall.at[w_part(node, x, i)], y_peer, "wy", f"wy{i}")

    def relay_w(i):
        rows = w_part((1 - y) * 2 + c, x, i)
        received(wall.at[rows], f"wy{i}")
        remote(wall.at[rows], wall.at[rows], x_peer, "wx", "wx")

    nw = WPARTS // 2
    for i in range(W_EARLY):
        send_w(i)

    def both(i, first, other):
        pair = jnp.concatenate([first(p, i) for p in range(2)], axis=1)
        return mm_t(pair, other[...])

    def own_tok(p, i):
        return tok_ref[:, col(p, c, i)]

    def their_tok(p, i):
        return tokx[p, :, quarter_rows(p, i)]

    for i in range(4):
        acc[i] = both(i, own_tok, cot_ref)

    def chip_sum(i):
        if i == 0:
            received(cotx, "cot")
        received(tokx.at[0, :, pl.ds(0, 2 * quarter)], f"tok{i}")
        return acc[i] + both(i, their_tok, cotx)

    def cs(s):
        return slice(s * HD, (s + 1) * HD)

    def pr(p):
        return slice(p * quarter, (p + 1) * quarter)

    st1 = {}
    for i in range(2):
        value = chip_sum(i).astype(BF16)
        for s in range(heads):
            for p in range(2):
                send1[i, p, s] = value[pr(p), cs(s)]
                st1[i, p, s] = copy_to(send1.at[i, p, s], recv1.at[i, p, s], towards[p][0], "first", f"first{i}{s}")
                if i == 0 or s == 0:
                    st1[i, p, s].start()
    remote(w_ref, wall.at[own_w], partner, "wp", "wp")
    for i in range(2, 4):
        acc[i] = chip_sum(i)

    to_z, bcast, sg2, sg1 = {}, {}, {}, {}

    def second(s):
        received(recv1.at[0, :, s], f"first0{s}")
        for p in range(2):
            send2[p, s] = (acc[2, pr(p), cs(s)] + recv1[0, p, s].astype(F32)).astype(BF16)
            remote(send2.at[p, s], recv2.at[p, s], towards[p][1], "second", f"second{s}")
        if s + 1 < heads:
            for p in range(2):
                st1[1, p, s + 1].start()

    def to_root(s):
        received(recv1.at[1, :, s], f"first1{s}")
        received(recv2.at[:, s], f"second{s}")
        for p in range(2):
            total = acc[3, pr(p), cs(s)] + recv1[1, p, s].astype(F32) + recv2[p, s].astype(F32)
            slot = lax.rem(z + 2 * zs - roots[p] - 1, zs)
            to_z[p, s] = copy_to(zsend.at[p, s], zrecv.at[s, slot], (node, roots[p] * 2 + x), f"z{p}", f"z{s}")

            @pl.when(z == roots[p])
            def _():
                acc[3, pr(p), cs(s)] = total

            @pl.when(z != roots[p])
            def _():
                zsend[p, s] = total.astype(BF16)
                to_z[p, s].start()

            mine = quarter_rows(p, 3)
            here = grad.at[p, s, mine]
            bcast[p, s] = [copy_to(here, here, (node, (roots[p] + d) % zs * 2 + x), "down", f"{('first1', 'second')[p]}{s}")
                           for d in range(1, zs)]
            sg1[p, s] = copy_to(here, here, towards[p][0], "gather", f"tok{s}")
            sg2[p, s] = copy_to(here, here, towards[p][1], "gather", f"first0{s}")

    def spread(p, s):
        sg2[p, s].start()
        sg1[p, s].start()

    def from_root(s):
        for p in range(2):
            @pl.when(z == roots[p])
            def _():
                total = acc[3, pr(p), cs(s)]
                received(zrecv.at[s], f"z{s}")
                for d in range(zs - 1):
                    total = total + zrecv[s, d].astype(F32)
                grad[p, s, quarter_rows(p, 3)] = total.astype(BF16)
                for cp in bcast[p, s]:
                    cp.start()
                spread(p, s)

    def at_leaf(s):
        for p in range(2):
            @pl.when(z != roots[p])
            def _():
                bcast[p, s][0].wait_recv()
                spread(p, s)

    def last_gather(s):
        received(grad.at[:, s, pl.ds(0, quarter)], f"first0{s}")
        for p in range(2):
            there = grad.at[p, s, quarter_rows(p, 2)]
            remote(there, there, towards[p][0], "gather", f"tok{s}")

    def input_rows(n, rows_of_w):
        rows = pl.ds(pl.multiple_of(n * block, block), block)
        out = lax.dot_general(cot_ref[...], rows_of_w, (((1,), (1,)), ((), ())), preferred_element_type=F32)
        igbuf[:, rows] = out.astype(BF16)

    def gathered(n):
        return wall[pl.ds(pl.multiple_of(n * block, block), block), :]

    def gram_of(h, p, bit):
        rows = pl.ds(pl.multiple_of(bit * half, half), half)
        g = grad[p, h, rows]
        return mm_t(g, g)

    for s in range(heads):
        second(s)
    for i in range(W_EARLY):
        relay_w(i)
    for i in range(W_EARLY, nw):
        send_w(i)
    input_rows(node, w_ref[...])
    received(w_ref, "wp")
    input_rows(y * 2 + 1 - c, gathered(y * 2 + 1 - c))

    def swap_w():
        received(wall.at[pl.ds(0, half)], "wx")
        y_w = pl.ds(pl.multiple_of(((1 - y) * 2 + c) * block, block), block)
        remote(wall.at[y_w], wall.at[y_w], partner, "wp", "wf")

    def finish_input():
        input_rows((1 - y) * 2 + c, gathered((1 - y) * 2 + c))
        received(w_ref, "wf")
        input_rows((1 - y) * 2 + 1 - c, gathered((1 - y) * 2 + 1 - c))

    def early_gram(s):
        early[s] = gram_of(s, 0, y) + gram_of(s, 1, x)

    def own_gram(s):
        received(grad.at[:, s, pl.ds(0, half)], f"tok{s}")
        gram_own[s] = early[s] + (gram_of(s, 0, 1 - y) + gram_of(s, 1, 1 - x))
        remote(gram_own.at[s], gram_in.at[s], partner, "gram", "gram")

    steps = {"z": to_root, "r": from_root, "l": at_leaf, "g": last_gather, "e": early_gram, "o": own_gram, "f": relay_w}
    extra = {"w": swap_w, "i": finish_input}
    for word in ORDER:
        if word in extra:
            extra[word]()
        else:
            steps[word[0]](int(word[1:]))

    rows_ref[...] = grad[y]
    received(gram_in, "gram")

    ii = lax.broadcasted_iota(jnp.int32, (HD, HD), 0)
    jj = lax.broadcasted_iota(jnp.int32, (HD, HD), 1)
    eye = (ii == jj).astype(F32)
    grams, totals, scales = [], [None] * heads, []
    for h in range(heads):
        raw = gram_own[h] + gram_in[h]
        squares = jnp.sum(jnp.sum(raw * eye, axis=1, keepdims=True), axis=0, keepdims=True)
        inverse = 1.0 / (jnp.sqrt(squares) + epsilon)
        scales.append(inverse)
        grams.append(raw * inverse * inverse)
    for step in range(NS_ITERS):
        rights = [right_form(g) for g in grams]
        squared = [product(left_form(g), r) for g, r in zip(grams, rights)]
        factors = [coef_a * eye + coef_b * g + coef_c * q for g, q in zip(grams, squared)]
        forms = [right_form(f) for f in factors]
        if step + 1 < NS_ITERS:
            halfway = [product(left_form(g), f) for g, f in zip(grams, forms)]
        if step == 0:
            totals = factors
        else:
            totals = [product(left_form(t), f) for t, f in zip(totals, forms)]
        if step + 1 < NS_ITERS:
            grams = [product(left_form(g), f) for g, f in zip(halfway, forms)]

    for h in range(heads):
        scaled = totals[h] * (scales[h] * (0.2 * math.sqrt(din)))
        form_ref[h] = jnp.concatenate(parts_of(scaled), axis=1)
    sent(cotx, "cot")
    sent(tokx, "tok")
    sent(send1, "first")
    sent(send2, "second")
    sent(wall.at[pl.ds(0, half)], "wy")
    sent(wall.at[pl.ds(0, half)], "wx")
    sent(wall.at[pl.ds(0, 2 * block)], "wp")
    sent(grad.at[:, :, pl.ds(0, 3 * quarter)], "gather")
    sent(gram_own, "gram")
    for p in range(2):
        @pl.when(z == roots[p])
        def _():
            sent(grad.at[0, :, pl.ds(0, 3 * quarter)], "down")

        @pl.when(z != roots[p])
        def _():
            sent(zsend.at[p], f"z{p}")


def finish(ig_ref, rows_ref, form_ref, ig_out, up_out, upbuf, sems):
    heads = form_ref.shape[0]
    step = upbuf.shape[0] // 4
    copies = [pltpu.make_async_copy(ig_ref, ig_out, sems.at[0])]
    copies[0].start()
    for i in range(4):
        part = pl.ds(i * step, step)
        for h in range(heads):
            upbuf[part, pl.ds(h * HD, HD)] = product(rows_ref[h, part], form_ref[h])
        copies.append(pltpu.make_async_copy(upbuf.at[part], up_out.at[part], sems.at[i + 1]))
        copies[-1].start()
    for cp in copies:
        cp.wait()


def fused(tokens, cotangent, value_weight, zs):
    tok, din = tokens.shape
    width = cotangent.shape[1]
    heads = width // HD
    block = din // 4
    quarter = block // 4
    nsend = 12
    nrecv = 1 + 4 + 4 * heads + WPARTS // 2 + 4
    vm, dma = pltpu.VMEM, pltpu.SemaphoreType.DMA
    held = pl.pallas_call(
        functools.partial(kernel, (width, heads, zs)),
        out_shape=(
            jax.ShapeDtypeStruct((tok, din), BF16),
            jax.ShapeDtypeStruct((heads, block, HD), BF16),
            jax.ShapeDtypeStruct((heads, HD, 2 * HD), BF16),
        ),
        in_specs=[pl.BlockSpec(memory_space=pl.ANY)] * 3,
        out_specs=(pl.BlockSpec(memory_space=pltpu.VMEM),) * 3,
        scratch_shapes=[
            vm((tok, din), BF16),
            vm((tok, width), BF16),
            vm((block, width), BF16),
            vm((2, tok, block), BF16),
            vm((tok, width), BF16),
            vm((din, width), BF16),
            vm((4, 2 * quarter, width), F32),
            vm((2, 2, heads, quarter, HD), BF16),
            vm((2, 2, heads, quarter, HD), BF16),
            vm((2, heads, quarter, HD), BF16),
            vm((2, heads, quarter, HD), BF16),
            vm((2, heads, quarter, HD), BF16),
            vm((heads, zs - 1, quarter, HD), BF16),
            vm((2, heads, block, HD), BF16),
            vm((heads, HD, HD), F32),
            vm((heads, HD, HD), F32),
            vm((heads, HD, HD), F32),
            dma((3,)),
            dma((nsend,)),
            dma((nrecv,)),
        ],
        compiler_params=pltpu.CompilerParams(collective_id=0, has_side_effects=True, vmem_limit_bytes=24 * 1024 * 1024),
    )(*(pltpu.with_memory_space_constraint(a, pltpu.HBM) for a in (tokens, cotangent, value_weight)))
    return pl.pallas_call(
        finish,
        out_shape=(jax.ShapeDtypeStruct((tok, din), BF16), jax.ShapeDtypeStruct((block, width), F32)),
        in_specs=[pl.BlockSpec(memory_space=pltpu.VMEM)] * 3,
        out_specs=(pl.BlockSpec(memory_space=pltpu.HBM),) * 2,
        scratch_shapes=[vm((block, width), F32), pltpu.SemaphoreType.DMA((5,))],
        compiler_params=pltpu.CompilerParams(vmem_limit_bytes=8 * 1024 * 1024),
    )(*held)


def general(tokens, cotangent, value_weight):
    width = value_weight.shape[1]
    din = tokens.shape[1]
    local_rows = value_weight.shape[0]
    heads = width // HD
    input_grad = lax.dot_general(
        cotangent,
        lax.all_gather(value_weight, "node", axis=0, tiled=True),
        (((1,), (1,)), ((), ())),
        preferred_element_type=F32,
    ).astype(BF16)
    partial_rows = lax.psum_scatter(
        lax.dot_general(tokens, cotangent, (((0,), (0,)), ((), ())), preferred_element_type=F32).astype(BF16),
        "node",
        scatter_dimension=0,
        tiled=True,
    ).astype(F32)
    gradient = lax.psum(partial_rows, "rep")
    blocks = gradient.reshape(local_rows, heads, HD)
    exact = functools.partial(jnp.einsum, precision=lax.Precision.HIGHEST)
    gram_raw = lax.psum(exact("rhi,rhj->hij", blocks, blocks), "node")
    divisor = jnp.sqrt(jnp.einsum("hii->h", gram_raw)) + epsilon
    gram = gram_raw / (divisor * divisor)[:, None, None]
    identity = jnp.broadcast_to(jnp.eye(HD, dtype=F32), (heads, HD, HD))
    total = identity
    for step in range(NS_ITERS):
        factor = coef_a * identity + coef_b * gram + coef_c * exact("hij,hjk->hik", gram, gram)
        total = exact("hij,hjk->hik", total, factor)
        if step + 1 < NS_ITERS:
            gram = exact("hji,hjk->hik", factor, exact("hij,hjk->hik", gram, factor))
    iterate = exact("rhi,hij->rhj", blocks / divisor[None, :, None], total)
    return input_grad, 0.2 * math.sqrt(din) * iterate.reshape(local_rows, width)


def solution(mesh):
    nodes, reps = mesh.shape["node"], mesh.shape["rep"]

    def per_device(tokens, cotangent, value_weight):
        zs = reps // 2
        fits = nodes == 4 and reps == 8 and tokens.shape[1] % (nodes * 4 * HD) == 0 and value_weight.shape[1] == 4 * HD
        if fits:
            return fused(tokens, cotangent, value_weight, zs)
        return general(tokens, cotangent, value_weight)

    return jax.shard_map(
        per_device,
        mesh=mesh,
        in_specs=(P(("node", "rep"), None), P(("node", "rep"), None), P("node", None)),
        out_specs=(P(("node", "rep"), None), P("node", None)),
        check_vma=False,
    )
```

time: 44.7 us -> 42.3 us (0.946)
  the two profiles are of different devices: /device:TPU:1 before, /device:TPU:0 now
where the time goes in v1:
time: 42.3 us; the launch traced here: 41.6 us
  Pallas kernels  41 us (97%)
  between operations  0.64 us (2%)
    pallas_call x1, Pallas kernels, fused(): pl.pallas_call(functools.partial(kernel, (width, heads, zs)), out_shape=(...  39.6 us
    pallas_call x1, Pallas kernels, fused(): pl.pallas_call(finish, out_shape=(jax.ShapeDtypeStruct((tok, din), BF16),...  1.36 us

profile of v1, /device:TPU:0, one launch (start us, length us, event | category | flops | bytes accessed | tf_op | source)
XLA Modules:
  0.0 41.6 jit_solution(16243033227400772642)
XLA Ops:
  0.6 39.6 %shard_map.50 = (bf16[256,2048]{1,0:T(8,128)(2,1)S(1)}, bf16[4,512,128]{2,1,0:T(8,128)(2,1)S(1)}, bf16[4,128,256]{2,1,0:T(8,128)(2,1)S(1)}) custom-call(bf16[256,2048]{1,0:T(8,128)(2,1)} %tok_hbm.1, bf16[256,512]{1,0:T(8,128)(2,1)} %cot_hbm.1, bf16[512,512]{1,0:T(8,128)(2,1)} %w_hbm.1), custom_call_target="tpu_custom_call" | custom-call | tf_op jit(solution)/shard_map/pallas_call | solution.py:366
  40.2 1.4 %shard_map.51 = (bf16[256,2048]{1,0:T(8,128)(2,1)}, f32[512,512]{1,0:T(8,128)}) custom-call(bf16[256,2048]{1,0:T(8,128)(2,1)S(1)} %get-tuple-element.5.ig_ref, bf16[4,512,128]{2,1,0:T(8,128)(2,1)S(1)} %get-tuple-element.6.rows_ref, bf16[4,128,256]{2,1,0:T(8,128)(2,1)S(1)} %get-tuple-element.7.form_ref), custom_call_target="tpu_custom_call" | custom-call | tf_op jit(solution)/shard_map/pallas_call | solution.py:399

commit v2 on v1

--- a/solution.py
+++ b/solution.py
@@ -11,8 +11,14 @@
 HD = 128
 NS_ITERS = 5
 WPARTS = 8
-W_EARLY = 1
-ORDER = ("z0", "z1", "z2", "r0", "z3", "f1", "r1", "f2", "r2", "f3", "l0", "r3", "l1", "g0", "l2", "g1", "e0", "l3", "g2", "e1", "g3", "w", "e2", "e3", "i", "o0", "o1", "o2", "o3")
+PIECES = 2
+AHEAD = 2
+SWAP_AT = 3
+ORDER = (
+    "z0", "z1", "z2", "z3", "f1", "z4", "z5", "r0", "z6", "r1", "z7", "r2", "r3", "l0", "r4", "f2",
+    "l1", "r5", "l2", "r6", "l3", "r7", "g0", "l4", "g1", "l5", "g2", "e0", "l6", "l7", "g3", "g4",
+    "e1", "g5", "g6", "e2", "g7", "w", "e3", "i", "o0", "o1", "o2", "o3",
+)
 
 coef_a = 3.4445
 coef_b = -4.775
@@ -55,6 +61,8 @@
     block = din // 4
     half, quarter = block // 2, block // 4
     wpart = block // WPARTS
+    chunks = heads * PIECES
+    rows_c = quarter // PIECES
 
     node, rep = lax.axis_index("node"), lax.axis_index("rep")
     y, c = node // 2, node % 2
@@ -95,6 +103,9 @@
         q = 1 - b1 if i % 2 == 0 else b1
         return h * half + q * quarter
 
+    def chunk_rows(p, i, t):
+        return pl.ds(pl.multiple_of(start_of(p, i) + t % PIECES * rows_c, rows_c), rows_c)
+
     def quarter_rows(p, i):
         return pl.ds(pl.multiple_of(start_of(p, i), quarter), quarter)
 
@@ -122,21 +133,29 @@
             remote(tok_ref.at[:, col(p, 1 - c, i)], tokx.at[p, :, quarter_rows(p, i)], partner, "tok", f"tok{i}")
     loads[2].wait()
 
-    def w_part(n, side, i):
-        return pl.ds(pl.multiple_of(n * block + side * half + i * wpart, wpart), wpart)
-
-    def send_w(i):
-        rows = pl.ds(pl.multiple_of(x * half + i * wpart, wpart), wpart)
-        remote(w_ref.at[rows], wall.at[w_part(node, x, i)], y_peer, "wy", f"wy{i}")
+    even = lax.rem(z, 2)
+    z_pair = (node, (z + 1 - 2 * even) * 2 + x)
+    w_at = [even, 1 - even, 2, 3]
+    other = (1 - y) * 2 + c
+
+    def w_rows(base, i, side):
+        return pl.ds(pl.multiple_of(base + side * half + w_at[i] * wpart, wpart), wpart)
+
+    def send_w(i, side, into):
+        remote(w_ref.at[w_rows(0, i, side)], wall.at[w_rows(node * block, i, side)], y_peer, "w", into)
+
+    def swap_w():
+        here = wall.at[w_rows(other * block, 0, x)]
+        received(here, "w0")
+        remote(here, here, z_pair, "w", "w1")
 
     def relay_w(i):
-        rows = w_part((1 - y) * 2 + c, x, i)
-        received(wall.at[rows], f"wy{i}")
-        remote(wall.at[rows], wall.at[rows], x_peer, "wx", "wx")
-
-    nw = WPARTS // 2
-    for i in range(W_EARLY):
-        send_w(i)
+        here = wall.at[w_rows(other * block, i, x)]
+        if i > 0:
+            received(here, f"w{i}")
+        remote(here, here, x_peer, "wx", "wx")
+
+    send_w(0, x, "w0")
 
     def both(i, first, other):
         pair = jnp.concatenate([first(p, i) for p in range(2)], axis=1)
@@ -160,86 +179,90 @@
     def cs(s):
         return slice(s * HD, (s + 1) * HD)
 
-    def pr(p):
-        return slice(p * quarter, (p + 1) * quarter)
+    def at(p, t):
+        start = p * quarter + t % PIECES * rows_c
+        return slice(start, start + rows_c), cs(t // PIECES)
 
     st1 = {}
     for i in range(2):
         value = chip_sum(i).astype(BF16)
-        for s in range(heads):
+        for t in range(chunks):
             for p in range(2):
-                send1[i, p, s] = value[pr(p), cs(s)]
-                st1[i, p, s] = copy_to(send1.at[i, p, s], recv1.at[i, p, s], towards[p][0], "first", f"first{i}{s}")
-                if i == 0 or s == 0:
-                    st1[i, p, s].start()
+                send1[i, p, t] = value[at(p, t)]
+                st1[i, p, t] = copy_to(send1.at[i, p, t], recv1.at[i, p, t], towards[p][0], "first", f"first{i}{t}")
+                if i == 0 or t < AHEAD:
+                    st1[i, p, t].start()
     remote(w_ref, wall.at[own_w], partner, "wp", "wp")
     for i in range(2, 4):
         acc[i] = chip_sum(i)
 
     to_z, bcast, sg2, sg1 = {}, {}, {}, {}
 
-    def second(s):
-        received(recv1.at[0, :, s], f"first0{s}")
-        for p in range(2):
-            send2[p, s] = (acc[2, pr(p), cs(s)] + recv1[0, p, s].astype(F32)).astype(BF16)
-            remote(send2.at[p, s], recv2.at[p, s], towards[p][1], "second", f"second{s}")
-        if s + 1 < heads:
+    def second(t):
+        received(recv1.at[0, :, t], f"first0{t}")
+        for p in range(2):
+            send2[p, t] = (acc[2][at(p, t)] + recv1[0, p, t].astype(F32)).astype(BF16)
+            remote(send2.at[p, t], recv2.at[p, t], towards[p][1], "second", f"second{t}")
+        if t + AHEAD < chunks:
             for p in range(2):
-                st1[1, p, s + 1].start()
-
-    def to_root(s):
-        received(recv1.at[1, :, s], f"first1{s}")
-        received(recv2.at[:, s], f"second{s}")
-        for p in range(2):
-            total = acc[3, pr(p), cs(s)] + recv1[1, p, s].astype(F32) + recv2[p, s].astype(F32)
+                st1[1, p, t + AHEAD].start()
+
+    def to_root(t):
+        h = t // PIECES
+        received(recv1.at[1, :, t], f"first1{t}")
+        received(recv2.at[:, t], f"second{t}")
+        for p in range(2):
+            rows, cols = at(p, t)
+            total = acc[3, rows, cols] + recv1[1, p, t].astype(F32) + recv2[p, t].astype(F32)
             slot = lax.rem(z + 2 * zs - roots[p] - 1, zs)
-            to_z[p, s] = copy_to(zsend.at[p, s], zrecv.at[s, slot], (node, roots[p] * 2 + x), f"z{p}", f"z{s}")
+            to_z[p, t] = copy_to(zsend.at[p, t], zrecv.at[t, slot], (node, roots[p] * 2 + x), f"z{p}", f"z{t}")
 
             @pl.when(z == roots[p])
             def _():
-                acc[3, pr(p), cs(s)] = total
+                acc[3, rows, cols] = total
 
             @pl.when(z != roots[p])
             def _():
-                zsend[p, s] = total.astype(BF16)
-                to_z[p, s].start()
-
-            mine = quarter_rows(p, 3)
-            here = grad.at[p, s, mine]
-            bcast[p, s] = [copy_to(here, here, (node, (roots[p] + d) % zs * 2 + x), "down", f"{('first1', 'second')[p]}{s}")
+                zsend[p, t] = total.astype(BF16)
+                to_z[p, t].start()
+
+            here = grad.at[p, h, chunk_rows(p, 3, t)]
+            bcast[p, t] = [copy_to(here, here, (node, (roots[p] + d) % zs * 2 + x), "down", f"{('first1', 'second')[p]}{t}")
                            for d in range(1, zs)]
-            sg1[p, s] = copy_to(here, here, towards[p][0], "gather", f"tok{s}")
-            sg2[p, s] = copy_to(here, here, towards[p][1], "gather", f"first0{s}")
-
-    def spread(p, s):
-        sg2[p, s].start()
-        sg1[p, s].start()
-
-    def from_root(s):
+            sg1[p, t] = copy_to(here, here, towards[p][0], "gather", f"tok{t}")
+            sg2[p, t] = copy_to(here, here, towards[p][1], "gather", f"first0{t}")
+
+    def from_root(t):
         for p in range(2):
             @pl.when(z == roots[p])
             def _():
-                total = acc[3, pr(p), cs(s)]
-                received(zrecv.at[s], f"z{s}")
+                rows, cols = at(p, t)
+                total = acc[3, rows, cols]
+                received(zrecv.at[t], f"z{t}")
                 for d in range(zs - 1):
-                    total = total + zrecv[s, d].astype(F32)
-                grad[p, s, quarter_rows(p, 3)] = total.astype(BF16)
-                for cp in bcast[p, s]:
+                    total = total + zrecv[t, d].astype(F32)
+                grad[p, t // PIECES, chunk_rows(p, 3, t)] = total.astype(BF16)
+                for cp in bcast[p, t]:
                     cp.start()
-                spread(p, s)
-
-    def at_leaf(s):
+                sg2[p, t].start()
+                sg1[p, t].start()
+
+    def at_leaf(t):
         for p in range(2):
             @pl.when(z != roots[p])
             def _():
-                bcast[p, s][0].wait_recv()
-                spread(p, s)
-
-    def last_gather(s):
-        received(grad.at[:, s, pl.ds(0, quarter)], f"first0{s}")
-        for p in range(2):
-            there = grad.at[p, s, quarter_rows(p, 2)]
-            remote(there, there, towards[p][0], "gather", f"tok{s}")
+                bcast[p, t][0].wait_recv()
+                sg2[p, t].start()
+        for p in range(2):
+            @pl.when(z != roots[p])
+            def _():
+                sg1[p, t].start()
+
+    def last_gather(t):
+        received(grad.at[:, 0, pl.ds(0, rows_c)], f"first0{t}")
+        for p in range(2):
+            there = grad.at[p, t // PIECES, chunk_rows(p, 2, t)]
+            remote(there, there, towards[p][0], "gather", f"tok{t}")
 
     def input_rows(n, rows_of_w):
         rows = pl.ds(pl.multiple_of(n * block, block), block)
@@ -254,19 +277,22 @@
         g = grad[p, h, rows]
         return mm_t(g, g)
 
-    for s in range(heads):
-        second(s)
-    for i in range(W_EARLY):
-        relay_w(i)
-    for i in range(W_EARLY, nw):
-        send_w(i)
+    for t in range(chunks):
+        second(t)
+        if t == SWAP_AT:
+            swap_w()
+    relay_w(0)
+    send_w(2, x, "w2")
+    send_w(3, x, "w3")
+    send_w(3, 1 - x, "w3")
     input_rows(node, w_ref[...])
     received(w_ref, "wp")
     input_rows(y * 2 + 1 - c, gathered(y * 2 + 1 - c))
 
-    def swap_w():
-        received(wall.at[pl.ds(0, half)], "wx")
-        y_w = pl.ds(pl.multiple_of(((1 - y) * 2 + c) * block, block), block)
+    def trade_w():
+        received(wall.at[pl.ds(0, 3 * wpart)], "wx")
+        received(wall.at[pl.ds(0, 2 * wpart)], "w3")
+        y_w = pl.ds(pl.multiple_of(other * block, block), block)
         remote(wall.at[y_w], wall.at[y_w], partner, "wp", "wf")
 
     def finish_input():
@@ -278,12 +304,13 @@
         early[s] = gram_of(s, 0, y) + gram_of(s, 1, x)
 
     def own_gram(s):
-        received(grad.at[:, s, pl.ds(0, half)], f"tok{s}")
+        for t in range(s * PIECES, (s + 1) * PIECES):
+            received(grad.at[:, 0, pl.ds(0, 2 * rows_c)], f"tok{t}")
         gram_own[s] = early[s] + (gram_of(s, 0, 1 - y) + gram_of(s, 1, 1 - x))
         remote(gram_own.at[s], gram_in.at[s], partner, "gram", "gram")
 
     steps = {"z": to_root, "r": from_root, "l": at_leaf, "g": last_gather, "e": early_gram, "o": own_gram, "f": relay_w}
-    extra = {"w": swap_w, "i": finish_input}
+    extra = {"w": trade_w, "i": finish_input}
     for word in ORDER:
         if word in extra:
             extra[word]()
@@ -308,11 +335,15 @@
         squared = [product(left_form(g), r) for g, r in zip(grams, rights)]
         factors = [coef_a * eye + coef_b * g + coef_c * q for g, q in zip(grams, squared)]
         forms = [right_form(f) for f in factors]
-        if step + 1 < NS_ITERS:
+        if step == 0:
             halfway = [product(left_form(g), f) for g, f in zip(grams, forms)]
+        elif step + 1 < NS_ITERS:
+            stacked = [jnp.concatenate([left_form(g), left_form(t)], axis=0) for g, t in zip(grams, totals)]
+            pairs_of = [product(a, f) for a, f in zip(stacked, forms)]
+            halfway, totals = [a[:HD] for a in pairs_of], [a[HD:] for a in pairs_of]
         if step == 0:
             totals = factors
-        else:
+        elif step + 1 == NS_ITERS:
             totals = [product(left_form(t), f) for t, f in zip(totals, forms)]
         if step + 1 < NS_ITERS:
             grams = [product(left_form(g), f) for g, f in zip(halfway, forms)]
@@ -324,8 +355,8 @@
     sent(tokx, "tok")
     sent(send1, "first")
     sent(send2, "second")
-    sent(wall.at[pl.ds(0, half)], "wy")
-    sent(wall.at[pl.ds(0, half)], "wx")
+    sent(wall.at[pl.ds(0, 5 * wpart)], "w")
+    sent(wall.at[pl.ds(0, 3 * wpart)], "wx")
     sent(wall.at[pl.ds(0, 2 * block)], "wp")
     sent(grad.at[:, :, pl.ds(0, 3 * quarter)], "gather")
     sent(gram_own, "gram")
@@ -361,7 +392,8 @@
     block = din // 4
     quarter = block // 4
     nsend = 12
-    nrecv = 1 + 4 + 4 * heads + WPARTS // 2 + 4
+    chunks, rows_c = heads * PIECES, quarter // PIECES
+    nrecv = 1 + max(4, chunks) + 4 * chunks + WPARTS // 2 + 4
     vm, dma = pltpu.VMEM, pltpu.SemaphoreType.DMA
     held = pl.pallas_call(
         functools.partial(kernel, (width, heads, zs)),
@@ -380,12 +412,12 @@
             vm((tok, width), BF16),
             vm((din, width), BF16),
             vm((4, 2 * quarter, width), F32),
-            vm((2, 2, heads, quarter, HD), BF16),
-            vm((2, 2, heads, quarter, HD), BF16),
-            vm((2, heads, quarter, HD), BF16),
-            vm((2, heads, quarter, HD), BF16),
-            vm((2, heads, quarter, HD), BF16),
-            vm((heads, zs - 1, quarter, HD), BF16),
+            vm((2, 2, chunks, rows_c, HD), BF16),
+            vm((2, 2, chunks, rows_c, HD), BF16),
+            vm((2, chunks, rows_c, HD), BF16),
+            vm((2, chunks, rows_c, HD), BF16),
+            vm((2, chunks, rows_c, HD), BF16),
+            vm((chunks, zs - 1, rows_c, HD), BF16),
             vm((2, heads, block, HD), BF16),
             vm((heads, HD, HD), F32),
             vm((heads, HD, HD), F32),

time: 42.3 us -> 40.3 us (0.953); the launches traced: 41.6 us -> 40.1 us
  Pallas kernels: 41 us -> 39.5 us
    pallas_call x1, Pallas kernels: 39.6 us -> 38.1 us  [fused(): pl.pallas_call(functools.partial(kernel, (width, heads, zs)), out_shape=(...]
where the time goes in v2:
time: 40.3 us; the launch traced here: 40.1 us
  Pallas kernels  39.5 us (98%)
  between operations  0.64 us (2%)
    pallas_call x1, Pallas kernels, fused(): pl.pallas_call(functools.partial(kernel, (width, heads, zs)), out_shape=(...  38.1 us
    pallas_call x1, Pallas kernels, fused(): pl.pallas_call(finish, out_shape=(jax.ShapeDtypeStruct((tok, din), BF16),...  1.36 us

profile of v2, /device:TPU:0, one launch (start us, length us, event | category | flops | bytes accessed | tf_op | source)
XLA Modules:
  0.0 40.1 jit_solution(2497072129116619054)
XLA Ops:
  0.6 38.1 %shard_map.50 = (bf16[256,2048]{1,0:T(8,128)(2,1)S(1)}, bf16[4,512,128]{2,1,0:T(8,128)(2,1)S(1)}, bf16[4,128,256]{2,1,0:T(8,128)(2,1)S(1)}) custom-call(bf16[256,2048]{1,0:T(8,128)(2,1)} %tok_hbm.1, bf16[256,512]{1,0:T(8,128)(2,1)} %cot_hbm.1, bf16[512,512]{1,0:T(8,128)(2,1)} %w_hbm.1), custom_call_target="tpu_custom_call" | custom-call | tf_op jit(solution)/shard_map/pallas_call | solution.py:398
  38.8 1.4 %shard_map.51 = (bf16[256,2048]{1,0:T(8,128)(2,1)}, f32[512,512]{1,0:T(8,128)}) custom-call(bf16[256,2048]{1,0:T(8,128)(2,1)S(1)} %get-tuple-element.5.ig_ref, bf16[4,512,128]{2,1,0:T(8,128)(2,1)S(1)} %get-tuple-element.6.rows_ref, bf16[4,128,256]{2,1,0:T(8,128)(2,1)S(1)} %get-tuple-element.7.form_ref), custom_call_target="tpu_custom_call" | custom-call | tf_op jit(solution)/shard_map/pallas_call | solution.py:431
